TPU v7x, 32 devices: a whole 2x2x4 slice. The times are simulated.
32 devices in a mesh: dp: 4 (over y, core), tensor: 8 (over z, x).
Axes of the slice: x: 2, y: 2, z: 4, core: 2. Of those that a mesh axis runs over, the one named last changes fastest.
Arguments:
- query_latent: bfloat16 [64, 1536], P(('dp', 'tensor')), may hold values from -40 to 40
- key_value_latent: bfloat16 [64, 512], P(('dp', 'tensor')), may hold values from -40 to 40
- query_gain: float32 [1536], replicated, may hold values from 0.5 to 1.5
- key_value_gain: float32 [512], replicated, may hold values from 0.5 to 1.5
- q_up: bfloat16 [1536, 3072], P(None, 'tensor'), may hold values from -0.625 to 0.625
- kv_up: bfloat16 [512, 4096], P(None, 'tensor'), may hold values from -1 to 1
- grad_q: bfloat16 [64, 3072], P('dp', 'tensor'), may hold values from -0.23925781 to 0.23925781
- grad_kv: bfloat16 [64, 4096], P('dp', 'tensor'), may hold values from -0.23925781 to 0.23925781
Outputs:
- query_latent_gradient: float32 [64, 1536], P(('dp', 'tensor'))
- key_value_latent_gradient: float32 [64, 512], P(('dp', 'tensor'))
- d_q_up: float32 [1536, 3072], P('dp', 'tensor')
- d_kv_up: float32 [512, 4096], P('dp', 'tensor')
All inputs are finite; a program needn't handle non-finite values.
Results may differ from a plain program's by a relative error of at most 0.0029.
Values may be sent and summed in bfloat16 or wider, within the bound.
No kernel may reach another device: no remote copies, remote signals or barrier semaphores. Data moves between devices by JAX's collectives and lax.ppermute only.
A program may use at most 64 MiB of HBM per device.

v0:
```python
import jax
import jax.numpy as jnp
from jax import lax
from jax.sharding import PartitionSpec as P

EPS = 1e-06


def apply_norm(raw, norm_gain):
    input_values = raw.astype(jnp.float32)
    inverse_norm = lax.rsqrt(jnp.mean(input_values * input_values, axis=-1, keepdims=True) + EPS)
    unit_input = input_values * inverse_norm
    return (unit_input, inverse_norm, (norm_gain * unit_input).astype(jnp.bfloat16))


def backward_of_norm(incoming_gradient, unit_input, inverse_norm, norm_gain):
    scaled_gradient = norm_gain * incoming_gradient
    mean_correction = jnp.mean(scaled_gradient * unit_input, axis=-1, keepdims=True)
    return inverse_norm * (scaled_gradient - unit_input * mean_correction)


def contract_rows(left, right):
    return lax.dot_general(
        left, right, (((0,), (0,)), ((), ())), preferred_element_type=jnp.float32
    )


def contract_cols(left, right):
    return lax.dot_general(
        left, right, (((1,), (1,)), ((), ())), preferred_element_type=jnp.float32
    )


def body(query_latent, key_value_latent, query_gain, key_value_gain, q_up, kv_up, grad_q, grad_kv):
    query_width = query_latent.shape[1]
    whole_q, whole_kv = (
        lax.all_gather(query_latent, "tensor", axis=0, tiled=True),
        lax.all_gather(key_value_latent, "tensor", axis=0, tiled=True),
    )
    part_q = contract_rows(apply_norm(whole_q, query_gain)[2], grad_q)
    part_kv = contract_rows(apply_norm(whole_kv, key_value_gain)[2], grad_kv)
    d_q_up, d_kv_up = (
        lax.psum_scatter(part_q, "dp", scatter_dimension=0, tiled=True),
        lax.psum_scatter(part_kv, "dp", scatter_dimension=0, tiled=True),
    )
    summed_products = lax.psum_scatter(
        jnp.concatenate((contract_cols(grad_q, q_up), contract_cols(grad_kv, kv_up)), axis=1),
        "tensor",
        scatter_dimension=0,
        tiled=True,
    )
    query_unit, query_inverse_norm, unused_item = apply_norm(query_latent, query_gain)
    key_value_unit, key_value_inverse_norm, unused_item = apply_norm(
        key_value_latent, key_value_gain
    )
    query_latent_gradient = backward_of_norm(
        summed_products[:, :query_width], query_unit, query_inverse_norm, query_gain
    )
    key_value_latent_gradient = backward_of_norm(
        summed_products[:, query_width:], key_value_unit, key_value_inverse_norm, key_value_gain
    )
    return (query_latent_gradient, key_value_latent_gradient, d_q_up, d_kv_up)


def solution(mesh):
    return jax.shard_map(
        body,
        mesh=mesh,
        in_specs=(
            P(("dp", "tensor"), None),
            P(("dp", "tensor"), None),
            P(),
            P(),
            P(None, "tensor"),
            P(None, "tensor"),
            P("dp", "tensor"),
            P("dp", "tensor"),
        ),
        out_specs=(
            P(("dp", "tensor"), None),
            P(("dp", "tensor"), None),
            P("dp", "tensor"),
            P("dp", "tensor"),
        ),
        check_vma=False,
    )
```

profile of v0, /device:TPU:0, one launch (start us, length us, event | category | flops | bytes accessed | tf_op | source)
XLA Modules:
  0.0 113.6 jit_solution(14444127462413539571)
XLA Ops:
  8.0 0.0 copy-start
  8.0 0.0 copy-start.1
  8.0 0.0 copy-start.4
  8.0 0.0 copy-start.6
  8.0 0.0 copy-start.7
  8.1 0.0 all-reduce.3.cloned.1.call-start
  8.1 1.2 %copy-done = bf16[1536,384]{1,0:T(8,128)(2,1)S(1)} copy-done((bf16[1536,384]{1,0:T(8,128)(2,1)S(1)}, bf16[1536,384]{1,0:T(8,128)(2,1)}, u32[]{:S(2)}) %copy-start) | copy-done | bytes 1179672
  9.3 1.1 fusion.18
  10.4 0.0 copy-done.1
  10.4 0.0 copy-done.4
  10.4 0.3 fusion.19
  10.6 0.7 pad_maximum_fusion
  11.3 0.0 copy-start.2
  11.3 0.0 all-reduce.3.cloned.1.call-update
  11.3 0.0 reduce-scatter.5.cloned.1.call-start
  11.4 0.0 copy-done.6
  11.4 27.9 %all-gather.1 = bf16[8,2,512]{2,1,0:T(2,128)(2,1)S(1)} all-gather(bf16[1,2,512]{2,1,0:T(2,128)(2,1)S(1)} %bitcast.10), channel_id=1, replica_groups=mesh['dp'=4,'tensor'=8] {'tensor'}, dimensions={0}, use_global_device_ids=true | all-gather | bytes 18432 | tf_op jit(solution)/shard_map/all_gather | solution.py:38
  39.3 0.1 multiply_reduce_fusion.1
  39.5 0.0 copy-done.7
  39.5 0.0 copy-start.3
  39.5 0.0 copy-start.5
  39.5 1.4 %fusion.3 = f32[512,512]{1,0:T(8,128)} fusion(bf16[16,512]{1,0:T(8,128)(2,1)S(1)} %copy-done.4, f32[16,512]{1,0:T(8,128)S(1)} %reshape.55, f32[16]{0:T(128)S(1)} %add_rsqrt_fusion, f32[512]{0:T(512)S(1)} %copy-done.7), kind=kOutput, calls=%fused_computation.8 | convolution fusion | flops 8413184 | bytes 1099840 | tf_op jit(solution)/shard_map/dot_general | solution.py:23
  40.9 0.0 reduce-scatter.5.cloned.1.call-update
  40.9 0.0 reduce-scatter.3.cloned.1.call-start
  41.0 0.0 copy-done.2
  41.0 30.8 %all-gather = bf16[8,2,1536]{2,1,0:T(2,128)(2,1)S(1)} all-gather(bf16[1,2,1536]{2,1,0:T(2,128)(2,1)S(1)} %bitcast.9), channel_id=1, replica_groups=mesh['dp'=4,'tensor'=8] {'tensor'}, dimensions={0}, use_global_device_ids=true | all-gather | bytes 55296 | tf_op jit(solution)/shard_map/all_gather | solution.py:37
  71.8 0.1 multiply_reduce_fusion
  71.9 0.0 copy-done.3
  71.9 0.0 copy-done.5
  71.9 2.0 %fusion = f32[1536,384]{1,0:T(8,128)} fusion(bf16[16,384]{1,0:T(8,128)(2,1)S(1)} %copy-done.5, f32[16,1536]{1,0:T(8,128)S(1)} %reshape.54, f32[16]{0:T(128)S(1)} %add_rsqrt_fusion.1, f32[1536]{0:T(1024)S(1)} %copy-done.3), kind=kOutput, calls=%fused_computation.3 | convolution fusion | flops 18948096 | bytes 2476096 | tf_op jit(solution)/shard_map/dot_general | solution.py:23
  73.9 0.0 copy-start.8
  73.9 0.0 reduce-scatter.3.cloned.1.call-update
  73.9 0.6 copy-done.8
  74.6 0.6 dynamic-slice
  75.8 0.1 fusion.17
  75.9 0.1 fusion.11
  76.1 9.4 %all-reduce.3.cloned.1.call-done = f32[16,2048]{1,0:T(8,128)} async-done(((f32[16,2048]{1,0:T(8,128)}), f32[16,2048]{1,0:T(8,128)}) %all-reduce.3.cloned.1.call-update) | async-done | bytes 131088
  85.5 0.9 fusion.14
  86.4 1.0 fusion.8
  87.4 1.4 %fusion.16 = f32[2,512]{1,0:T(2,128)} fusion(bf16[2,512]{1,0:T(2,128)(2,1)S(1)} %copy-done.6, f32[2]{0:T(128)S(1)} %broadcast_multiply_fusion, f32[2]{0:T(128)S(1)} %add_rsqrt_fusion.2, f32[16,2048]{1,0:T(8,128)} %all-reduce.3.cloned.1.call-done, u32[]{:T(128)S(6)} %multiply.37, u32[]{:T(128)S(6)} %convert, f32[512]{0:T(512)S(1)} %copy-done.7), kind=kLoop, calls=%fused_computation.26 | loop fusion | flops 6144 | bytes 12312 | tf_op jit(solution)/shard_map/mul | solution.py:19
  88.8 1.5 %fusion.10 = f32[2,1536]{1,0:T(2,128)} fusion(bf16[2,1536]{1,0:T(2,128)(2,1)S(1)} %copy-done.2, f32[16,2048]{1,0:T(8,128)} %all-reduce.3.cloned.1.call-done, u32[]{:T(128)S(6)} %multiply.37, f32[2]{0:T(128)S(1)} %broadcast_multiply_fusion.1, f32[2]{0:T(128)S(1)} %add_rsqrt_fusion.3, f32[1536]{0:T(1024)S(1)} %copy-done.3), kind=kLoop, calls=%fused_computation.17 | loop fusion | flops 18432 | bytes 36884 | tf_op jit(solution)/shard_map/mul | solution.py:19
  90.2 0.0 reduce-scatter.5.cloned.1.call-done
  90.3 15.9 %reduce-scatter.3.cloned.1.call-done = f32[384,384]{1,0:T(8,128)} async-done(((f32[1536,384]{1,0:T(8,128)}), f32[384,384]{1,0:T(8,128)}) %reduce-scatter.3.cloned.1.call-update) | async-done | bytes 589840 | tf_op jit(solution)/shard_map/reduce_scatter | solution.py:43
  (8 shorter events, 0.1 us)
Async XLA Ops:
  8.0 1.3 %copy-start = (bf16[1536,384]{1,0:T(8,128)(2,1)S(1)}, bf16[1536,384]{1,0:T(8,128)(2,1)}, u32[]{:S(2)}) copy-start(bf16[1536,384]{1,0:T(8,128)(2,1)} %param.12) | copy-start | bytes 3538948
  8.0 2.4 %copy-start.1 = (bf16[512,512]{1,0:T(8,128)(2,1)S(1)}, bf16[512,512]{1,0:T(8,128)(2,1)}, u32[]{:S(2)}) copy-start(bf16[512,512]{1,0:T(8,128)(2,1)} %param.13) | copy-start | bytes 1572868
  8.0 2.4 %copy-start.4 = (bf16[16,512]{1,0:T(8,128)(2,1)S(1)}, bf16[16,512]{1,0:T(8,128)(2,1)}, u32[]{:S(2)}) copy-start(bf16[16,512]{1,0:T(8,128)(2,1)} %param.15) | copy-start | bytes 49156
  8.0 3.4 %copy-start.6 = (bf16[2,512]{1,0:T(2,128)(2,1)S(1)}, bf16[2,512]{1,0:T(2,128)(2,1)}, u32[]{:S(2)}) copy-start(bf16[2,512]{1,0:T(2,128)(2,1)} %param.9) | copy-start | bytes 6148
  8.0 31.4 %copy-start.7 = (f32[512]{0:T(512)S(1)}, f32[512]{0:T(512)}, u32[]{:S(2)}) copy-start(f32[512]{0:T(512)} %param.11) | copy-start | bytes 6148
  8.1 77.4 %all-reduce.3.cloned.1.call-start = ((), (), s32[]{:S(2)}) async-start(), calls=%async_computation.4 | async-start | bytes 262144
  11.3 29.6 %copy-start.2 = (bf16[2,1536]{1,0:T(2,128)(2,1)S(1)}, bf16[2,1536]{1,0:T(2,128)(2,1)}, u32[]{:S(2)}) copy-start(bf16[2,1536]{1,0:T(2,128)(2,1)} %param.8) | copy-start | bytes 18436
  11.3 78.9 %reduce-scatter.5.cloned.1.call-start = ((), (), s32[]{:S(2)}) async-start(), calls=%async_computation.3 | async-start | bytes 1310720 | tf_op jit(solution)/shard_map/reduce_scatter | solution.py:44
  39.5 32.4 %copy-start.3 = (f32[1536]{0:T(1024)S(1)}, f32[1536]{0:T(1024)}, u32[]{:S(2)}) copy-start(f32[1536]{0:T(1024)} %param.10) | copy-start | bytes 18436
  39.5 32.4 %copy-start.5 = (bf16[16,384]{1,0:T(8,128)(2,1)S(1)}, bf16[16,384]{1,0:T(8,128)(2,1)}, u32[]{:S(2)}) copy-start(bf16[16,384]{1,0:T(8,128)(2,1)} %param.14) | copy-start | bytes 36868
  40.9 65.2 %reduce-scatter.3.cloned.1.call-start = ((), (), s32[]{:S(2)}) async-start(), calls=%async_computation.2 | async-start | bytes 2949120 | tf_op jit(solution)/shard_map/reduce_scatter | solution.py:43
  73.9 0.7 copy-start.8
Sparse Core Ops, SparseCore 0:
  12.2 73.2 all-reduce.2
Sparse Core Ops, SparseCore 1:
  41.0 24.1 reduce-scatter.4
  74.0 32.0 reduce-scatter.2
where the time goes:
time: 114 us
  blocking collectives  58.7 us (51%)
  waiting for transfers between devices  25.3 us (22%)
  between operations  16.3 us (14%)
  other arithmetic  5.96 us (5%)
  matrix products  4.73 us (4%)
  local copies, waits for them, and re-layouts  2.45 us (2%)
    all_gather x1, blocking collectives, body(): lax.all_gather(query_latent, 'tensor', axis=0, tiled=True)  30.8 us
    all_gather x1, blocking collectives, body(): lax.all_gather(key_value_latent, 'tensor', axis=0, tiled=True)  27.9 us
    reduce_scatter x1, waiting for transfers between devices, body(): lax.psum_scatter(part_q, 'dp', scatter_dimension=0, tiled=True)  15.9 us
    unnamed x4, waiting for transfers between devices  9.45 us
    dot_general x2, matrix products, contract_rows(): lax.dot_general(left, right, (((0,), (0,)), ((), ())), preferred_element_...  3.37 us
    mul x2, other arithmetic, backward_of_norm(): return inverse_norm * (scaled_gradient - unit_input * mean_correction)  2.87 us
    unnamed x19, local copies, waits for them, and re-layouts  2.42 us
  transfers between devices with their start and end apart: 3, of which 2 were waited for; matrix products, arithmetic and copies ran while one was open for 8% of the time, Pallas kernels for 0%

commit v1 on v0

v1 whole, which is shorter than its diff:
```python
import functools

import jax
import jax.numpy as jnp
from jax import lax
from jax.experimental import pallas as pl
from jax.experimental.pallas import tpu as pltpu
from jax.sharding import PartitionSpec as P

EPS = 1e-06
CHUNKS = 3
VMEM = 16 * 1024 * 1024


def dp_pairs(size, step):
    if size & (size - 1) == 0:
        return [(i, i ^ step) for i in range(size)]
    return [(i, (i + step) % size) for i in range(size)]


def dp_source(size, step, me):
    if size & (size - 1) == 0:
        return jnp.bitwise_xor(me, step)
    return lax.rem(me + size - step, size)


def unit_of(raw):
    values = raw.astype(jnp.float32)
    inverse = lax.rsqrt(jnp.mean(values * values, axis=-1, keepdims=True) + EPS)
    return values * inverse, inverse


def contract_cols(left, right):
    return lax.dot_general(
        left, right, (((1,), (1,)), ((), ())), preferred_element_type=jnp.float32
    )


def contract_rows(left, right):
    return lax.dot_general(
        left, right, (((0,), (0,)), ((), ())), preferred_element_type=jnp.float32
    )


def first_kernel(n_dp, n_tensor, chunks, *refs):
    sources, (part, latent, grads), rest = refs[:8], refs[8:11], refs[11:]
    held, sems = rest[:8], rest[8]
    q_lat, kv_lat, q_gain, kv_gain, q_up, kv_up, grad_q, grad_kv = held
    own, q_width = q_lat.shape
    kv_width = kv_lat.shape[1]
    q_cols = grad_q.shape[1]
    q_rows, kv_rows = q_width // n_dp, kv_width // n_dp
    step = q_width // chunks

    def fetch(i):
        return pltpu.make_async_copy(sources[i], held[i], sems.at[i])

    def fetch_rows(c):
        at = pl.ds(c * step, step)
        return pltpu.make_async_copy(sources[4].at[at], q_up.at[at], sems.at[8 + c])

    for i in (0, 1, 2, 3, 6, 7, 5):
        fetch(i).start()
    for c in range(chunks):
        fetch_rows(c).start()
    for i in (0, 1, 2, 3):
        fetch(i).wait()
    q_normed = (q_gain[...][None] * unit_of(q_lat[...])[0]).astype(jnp.bfloat16)
    kv_normed = (kv_gain[...][None] * unit_of(kv_lat[...])[0]).astype(jnp.bfloat16)
    for d in range(n_dp):
        piece = jnp.concatenate(
            (q_normed[:, d * q_rows : (d + 1) * q_rows], kv_normed[:, d * kv_rows : (d + 1) * kv_rows]), axis=1
        )
        latent[d * n_tensor : (d + 1) * n_tensor] = jnp.broadcast_to(piece[None], (n_tensor,) + piece.shape)
    for i in (6, 7):
        fetch(i).wait()
    grads[:, :q_cols] = grad_q[...]
    grads[:, q_cols:] = grad_kv[...]

    def put(value, at):
        for t in range(n_tensor):
            part[t, :, at : at + value.shape[1]] = value[t * own : (t + 1) * own]

    fetch(5).wait()
    put(contract_cols(grad_kv[...], kv_up[...]), q_width)
    for c in range(chunks):
        fetch_rows(c).wait()
        put(contract_cols(grad_q[...], q_up[c * step : (c + 1) * step]), c * step)


def latent_kernel(part, q_lat, kv_lat, q_gain, kv_gain, q_out, kv_out):
    q_width = q_lat.shape[1]
    summed = jnp.sum(part[...], axis=0)
    for out, raw, gain, incoming in (
        (q_out, q_lat, q_gain, summed[:, :q_width]),
        (kv_out, kv_lat, kv_gain, summed[:, q_width:]),
    ):
        unit, inverse = unit_of(raw[...])
        scaled = gain[...][None] * incoming
        out[...] = inverse * (scaled - unit * jnp.mean(scaled * unit, axis=-1, keepdims=True))


def weight_kernel(n_dp, latent, *refs):
    grads, (q_out, kv_out) = refs[:-2], refs[-2:]
    me = lax.axis_index("dp")
    tokens = grads[0].shape[0]
    q_rows, q_cols = q_out.shape
    order = []
    for step in range(n_dp):
        start = pl.multiple_of(dp_source(n_dp, step, me) * tokens, tokens)
        order.append(latent[pl.ds(start, tokens), :])
    normed = jnp.concatenate(order, axis=0)
    every = jnp.concatenate([g[...] for g in grads], axis=0)
    q_out[...] = contract_rows(normed[:, :q_rows], every[:, :q_cols])
    kv_out[...] = contract_rows(normed[:, q_rows:], every[:, q_cols:])


def struct(shape, dtype=jnp.float32):
    return jax.ShapeDtypeStruct(shape, dtype)


def cost(flops, nbytes):
    return pl.CostEstimate(flops=flops, bytes_accessed=nbytes, transcendentals=0)


def body(n_dp, n_tensor, q_lat, kv_lat, q_gain, kv_gain, q_up, kv_up, grad_q, grad_kv):
    own, q_width = q_lat.shape
    kv_width = kv_lat.shape[1]
    tokens, q_cols = grad_q.shape
    kv_cols = grad_kv.shape[1]
    q_rows, kv_rows = q_width // n_dp, kv_width // n_dp
    rows, width = q_rows + kv_rows, q_width + kv_width
    inputs = (q_lat, kv_lat, q_gain, kv_gain, q_up, kv_up, grad_q, grad_kv)
    part, latent, grads = pl.pallas_call(
        functools.partial(first_kernel, n_dp, n_tensor, CHUNKS),
        in_specs=[pl.BlockSpec(memory_space=pltpu.HBM)] * 8,
        scratch_shapes=[pltpu.VMEM(x.shape, x.dtype) for x in inputs]
        + [pltpu.SemaphoreType.DMA((8 + CHUNKS,))],
        out_shape=(
            struct((n_tensor, own, width)),
            struct((n_dp * n_tensor, own, rows), jnp.bfloat16),
            struct((tokens, q_cols + kv_cols), jnp.bfloat16),
        ),
        cost_estimate=cost(2 * tokens * (q_cols * q_width + kv_cols * kv_width), 4000000),
        compiler_params=pltpu.CompilerParams(vmem_limit_bytes=VMEM),
        name="first",
    )(*[pltpu.with_memory_space_constraint(x, pltpu.HBM) for x in inputs])
    part = lax.all_to_all(part, "tensor", 0, 0)
    latent = lax.all_to_all(latent, ("dp", "tensor"), 0, 0)
    all_grads = [grads] + [lax.ppermute(grads, "dp", dp_pairs(n_dp, s)) for s in range(1, n_dp)]
    q_out, kv_out = pl.pallas_call(
        latent_kernel,
        out_shape=(struct(q_lat.shape), struct(kv_lat.shape)),
        cost_estimate=cost(10000, 200000),
        compiler_params=pltpu.CompilerParams(vmem_limit_bytes=VMEM),
        name="latent",
    )(part, q_lat, kv_lat, q_gain, kv_gain)
    q_weight, kv_weight = pl.pallas_call(
        functools.partial(weight_kernel, n_dp),
        out_shape=(struct((q_rows, q_cols)), struct((kv_rows, kv_cols))),
        cost_estimate=cost(2 * n_dp * tokens * (q_rows * q_cols + kv_rows * kv_cols), 1000000),
        compiler_params=pltpu.CompilerParams(vmem_limit_bytes=VMEM),
        name="weight",
    )(latent.reshape(n_dp * tokens, rows), *all_grads)
    return q_out, kv_out, q_weight, kv_weight


def solution(mesh):
    n_dp, n_tensor = mesh.shape["dp"], mesh.shape["tensor"]
    return jax.shard_map(
        functools.partial(body, n_dp, n_tensor),
        mesh=mesh,
        in_specs=(
            P(("dp", "tensor"), None),
            P(("dp", "tensor"), None),
            P(),
            P(),
            P(None, "tensor"),
            P(None, "tensor"),
            P("dp", "tensor"),
            P("dp", "tensor"),
        ),
        out_specs=(
            P(("dp", "tensor"), None),
            P(("dp", "tensor"), None),
            P("dp", "tensor"),
            P("dp", "tensor"),
        ),
        check_vma=False,
    )
```

time: 114 us -> 29.9 us (0.26)
  blocking collectives: 58.7 us -> 14.4 us
  waiting for transfers between devices: 25.3 us -> 4.31 us
  between operations: 16.3 us -> 0.7 us
  other arithmetic: 5.96 us -> 0 us
  starting transfers between devices: 0.13 us -> 5.3 us
  Pallas kernels: 0 us -> 4.83 us
  matrix products: 4.73 us -> 0 us
  local copies, waits for them, and re-layouts: 2.45 us -> 0.05 us
    all_gather x2 -> x0, blocking collectives: 58.7 us -> none  [the longest x1 30.8 us: body(): lax.all_gather(query_latent, 'tensor', axis=0, tiled=True)]
    reduce_scatter x2 -> x0, waiting for transfers between devices: 15.9 us -> none  [the longest x1 15.9 us: body(): lax.psum_scatter(part_q, 'dp', scatter_dimension=0, tiled=True)]
    all_to_all x0 -> x1, blocking collectives: none -> 14.4 us  [body(): latent = lax.all_to_all(latent, ('dp', 'tensor'), 0, 0)]
    unnamed x4 -> x0, waiting for transfers between devices: 9.45 us -> none
    pallas_call x0 -> x3, Pallas kernels: none -> 4.83 us  [the longest x1 2.82 us: body(): pl.pallas_call(functools.partial(first_kernel, n_dp, n_tensor, CHUNKS), i...]
    dot_general x4 -> x0, matrix products: 4.73 us -> none  [the longest x2 3.37 us: contract_rows(): lax.dot_general(left, right, (((0,), (0,)), ((), ())), preferred_element_...]
    all_to_all x0 -> x1, starting transfers between devices: none -> 3.37 us  [body(): part = lax.all_to_all(part, 'tensor', 0, 0)]
    mul x2 -> x0, other arithmetic: 2.87 us -> none  [backward_of_norm(): return inverse_norm * (scaled_gradient - unit_input * mean_correction)]
  transfers between devices with their start and end apart: 3 -> 4, of which waited for: 2 -> 3; matrix products, arithmetic and copies ran while one was open for 8% -> 0% of each run, Pallas kernels for 0% -> 4%
where the time goes in v1:
time: 29.9 us; the launch traced here: 29.6 us
  blocking collectives  14.4 us (48%)
  starting transfers between devices  5.3 us (18%)
  Pallas kernels  4.83 us (16%)
  waiting for transfers between devices  4.31 us (14%)
  between operations  0.7 us (2%)
    all_to_all x1, blocking collectives, body(): latent = lax.all_to_all(latent, ('dp', 'tensor'), 0, 0)  14.4 us
    all_to_all x1, starting transfers between devices, body(): part = lax.all_to_all(part, 'tensor', 0, 0)  3.37 us
    pallas_call x1, Pallas kernels, body(): pl.pallas_call(functools.partial(first_kernel, n_dp, n_tensor, CHUNKS), i...  2.82 us
    ppermute x3, waiting for transfers between devices, body(): lax.ppermute(grads, 'dp', dp_pairs(n_dp, s))  2.32 us
    all_to_all x1, waiting for transfers between devices, body(): part = lax.all_to_all(part, 'tensor', 0, 0)  1.99 us
    ppermute x3, starting transfers between devices, body(): lax.ppermute(grads, 'dp', dp_pairs(n_dp, s))  1.93 us
    pallas_call x1, Pallas kernels, body(): pl.pallas_call(functools.partial(weight_kernel, n_dp), out_shape=(struct(...  1.2 us
    pallas_call x1, Pallas kernels, body(): pl.pallas_call(latent_kernel, out_shape=(struct(q_lat.shape), struct(kv_l...  0.81 us
  transfers between devices with their start and end apart: 4, of which 3 were waited for; matrix products, arithmetic and copies ran while one was open for 0% of the time, Pallas kernels for 4%

profile of v1, /device:TPU:0, one launch (start us, length us, event | category | flops | bytes accessed | tf_op | source)
XLA Modules:
  0.0 29.6 jit_solution(10340054434281635943)
XLA Ops:
  0.6 0.0 copy-start.3
  0.6 0.0 copy-start
  0.7 0.0 copy-start.2
  0.7 0.0 copy-start.1
  0.7 2.8 %first.1 = (f32[8,2,2048]{2,1,0:T(2,128)}, bf16[32,2,512]{2,1,0:T(2,128)(2,1)S(1)}, bf16[16,896]{1,0:T(8,128)(2,1)S(1)}) custom-call(bf16[2,1536]{1,0:T(2,128)(2,1)} %q_lat.1, bf16[2,512]{1,0:T(2,128)(2,1)} %kv_lat.1, f32[1536]{0:T(1024)} %q_gain.1, f32[512]{0:T(512)} %kv_gain.1, bf16[1536,384]{1,0:T(8,128)(2,1)} %refs_4_.1, bf16[512,512]{1,0:T(8,128)(2,1)} %refs_5_.1, ...), custom_call_target="tpu_custom_call" | custom-call | flops 27262976 | bytes 4000000 | tf_op jit(solution)/shard_map/first/pallas_call | solution.py:134
  3.5 14.4 %all_to_all.10 = bf16[32,2,512]{2,1,0:T(2,128)(2,1)S(1)} all-to-all(bf16[32,2,512]{2,1,0:T(2,128)(2,1)S(1)} %get-tuple-element.14), channel_id=1, replica_groups=mesh['dp'=4,'tensor'=8] {'dp','tensor'}, dimensions={0} | all-to-all | bytes 131072 | tf_op jit(solution)/shard_map/all_to_all | solution.py:149
  17.9 3.4 %all-to-all-start = ((f32[8,2,2048]{2,1,0:T(2,128)}), f32[8,2,2048]{2,1,0:T(2,128)S(1)}, u32[]{:S(2)}, u32[]{:S(2)}) async-start(f32[8,2,2048]{2,1,0:T(2,128)} %get-tuple-element.11), calls=%async_computation | async-start | bytes 262144 | tf_op jit(solution)/shard_map/all_to_all | solution.py:148
  21.3 0.3 %collective-permute-start.2 = (bf16[16,896]{1,0:T(8,128)(2,1)S(1)}, bf16[16,896]{1,0:T(8,128)(2,1)S(1)}, u32[]{:S(2)}, u32[]{:S(2)}) collective-permute-start(bf16[16,896]{1,0:T(8,128)(2,1)S(1)} %get-tuple-element.15.refs_0_), channel_id=1, source_target_pairs={{0,24},{8,16},{16,8},{24,0},{1,25},{9,17},{17,9},{25,1},{2,26},{10... | collective-permute-start | bytes 86024 | tf_op jit(solution)/shard_map/ppermute | solution.py:150
  21.6 1.5 %collective-permute-start.1 = (bf16[16,896]{1,0:T(8,128)(2,1)S(1)}, bf16[16,896]{1,0:T(8,128)(2,1)S(1)}, u32[]{:S(2)}, u32[]{:S(2)}) collective-permute-start(bf16[16,896]{1,0:T(8,128)(2,1)S(1)} %get-tuple-element.15.refs_0_), channel_id=1, source_target_pairs={{0,16},{8,24},{16,0},{24,8},{1,17},{9,25},{17,1},{25,9},{2,18},{10... | collective-permute-start | bytes 86024 | tf_op jit(solution)/shard_map/ppermute | solution.py:150
  23.1 0.1 collective-permute-start
  23.2 1.4 %collective-permute-done.2.refs_3_ = bf16[16,896]{1,0:T(8,128)(2,1)S(1)} collective-permute-done((bf16[16,896]{1,0:T(8,128)(2,1)S(1)}, bf16[16,896]{1,0:T(8,128)(2,1)S(1)}, u32[]{:S(2)}, u32[]{:S(2)}) %collective-permute-start.2) | collective-permute-done | bytes 28704 | tf_op jit(solution)/shard_map/ppermute | solution.py:150
  24.7 0.9 %collective-permute-done.1.refs_2_ = bf16[16,896]{1,0:T(8,128)(2,1)S(1)} collective-permute-done((bf16[16,896]{1,0:T(8,128)(2,1)S(1)}, bf16[16,896]{1,0:T(8,128)(2,1)S(1)}, u32[]{:S(2)}, u32[]{:S(2)}) %collective-permute-start.1) | collective-permute-done | bytes 28704 | tf_op jit(solution)/shard_map/ppermute | solution.py:150
  25.6 0.0 collective-permute-done.refs_1_
  25.6 1.2 %weight.1 = (f32[384,384]{1,0:T(8,128)}, f32[128,512]{1,0:T(8,128)}) custom-call(bf16[64,512]{1,0:T(8,128)(2,1)S(1)} %reshape.11.latent, bf16[16,896]{1,0:T(8,128)(2,1)S(1)} %get-tuple-element.15.refs_0_, bf16[16,896]{1,0:T(8,128)(2,1)S(1)} %collective-permute-done.refs_1_, bf16[16,896]{1,0:T(8,128)(2,1)S(1)} %collective-permute-done.1.refs_2_, ...), custom_call_target="tpu_custom_call" | custom-call | flops 27262976 | bytes 1000000 | tf_op jit(solution)/shard_map/weight/pallas_call | solution.py:158
  26.8 2.0 %all-to-all-done.part = f32[8,2,2048]{2,1,0:T(2,128)S(1)} async-done(((f32[8,2,2048]{2,1,0:T(2,128)}), f32[8,2,2048]{2,1,0:T(2,128)S(1)}, u32[]{:S(2)}, u32[]{:S(2)}) %all-to-all-start) | async-done | bytes 131104 | tf_op jit(solution)/shard_map/all_to_all | solution.py:148
  28.8 0.0 copy-done.3
  28.8 0.0 copy-done
  28.8 0.0 copy-done.2
  28.8 0.0 copy-done.1
  28.8 0.8 %latent.1 = (f32[2,1536]{1,0:T(2,128)}, f32[2,512]{1,0:T(2,128)}) custom-call(f32[8,2,2048]{2,1,0:T(2,128)S(1)} %all-to-all-done.part, bf16[2,1536]{1,0:T(2,128)(2,1)S(1)} %copy-done.1, bf16[2,512]{1,0:T(2,128)(2,1)S(1)} %copy-done.2, f32[1536]{0:T(1024)S(1)} %copy-done, f32[512]{0:T(512)S(1)} %copy-done.3), custom_call_target="tpu_custom_call" | custom-call | flops 10000 | bytes 200000 | tf_op jit(solution)/shard_map/latent/pallas_call | solution.py:151
  (1 shorter events, 0.0 us)
Async XLA Ops:
  0.6 28.1 %copy-start.3 = (f32[512]{0:T(512)S(1)}, f32[512]{0:T(512)}, u32[]{:S(2)}) copy-start(f32[512]{0:T(512)} %kv_gain.1) | copy-start | bytes 6148
  0.6 28.1 %copy-start = (f32[1536]{0:T(1024)S(1)}, f32[1536]{0:T(1024)}, u32[]{:S(2)}) copy-start(f32[1536]{0:T(1024)} %q_gain.1) | copy-start | bytes 18436
  0.7 28.1 %copy-start.2 = (bf16[2,512]{1,0:T(2,128)(2,1)S(1)}, bf16[2,512]{1,0:T(2,128)(2,1)}, u32[]{:S(2)}) copy-start(bf16[2,512]{1,0:T(2,128)(2,1)} %kv_lat.1) | copy-start | bytes 6148
  0.7 28.1 %copy-start.1 = (bf16[2,1536]{1,0:T(2,128)(2,1)S(1)}, bf16[2,1536]{1,0:T(2,128)(2,1)}, u32[]{:S(2)}) copy-start(bf16[2,1536]{1,0:T(2,128)(2,1)} %q_lat.1) | copy-start | bytes 18436
  17.9 10.9 %all-to-all-start = ((f32[8,2,2048]{2,1,0:T(2,128)}), f32[8,2,2048]{2,1,0:T(2,128)S(1)}, u32[]{:S(2)}, u32[]{:S(2)}) async-start(f32[8,2,2048]{2,1,0:T(2,128)} %get-tuple-element.11), calls=%async_computation | async-start | bytes 262144 | tf_op jit(solution)/shard_map/all_to_all | solution.py:148
  21.3 3.4 %collective-permute-start.2 = (bf16[16,896]{1,0:T(8,128)(2,1)S(1)}, bf16[16,896]{1,0:T(8,128)(2,1)S(1)}, u32[]{:S(2)}, u32[]{:S(2)}) collective-permute-start(bf16[16,896]{1,0:T(8,128)(2,1)S(1)} %get-tuple-element.15.refs_0_), channel_id=1, source_target_pairs={{0,24},{8,16},{16,8},{24,0},{1,25},{9,17},{17,9},{25,1},{2,26},{10... | collective-permute-start | bytes 86024 | tf_op jit(solution)/shard_map/ppermute | solution.py:150
  21.6 4.0 %collective-permute-start.1 = (bf16[16,896]{1,0:T(8,128)(2,1)S(1)}, bf16[16,896]{1,0:T(8,128)(2,1)S(1)}, u32[]{:S(2)}, u32[]{:S(2)}) collective-permute-start(bf16[16,896]{1,0:T(8,128)(2,1)S(1)} %get-tuple-element.15.refs_0_), channel_id=1, source_target_pairs={{0,16},{8,24},{16,0},{24,8},{1,17},{9,25},{17,1},{25,9},{2,18},{10... | collective-permute-start | bytes 86024 | tf_op jit(solution)/shard_map/ppermute | solution.py:150
  23.1 2.5 %collective-permute-start = (bf16[16,896]{1,0:T(8,128)(2,1)S(1)}, bf16[16,896]{1,0:T(8,128)(2,1)S(1)}, u32[]{:S(2)}, u32[]{:S(2)}) collective-permute-start(bf16[16,896]{1,0:T(8,128)(2,1)S(1)} %get-tuple-element.15.refs_0_), channel_id=1, source_target_pairs={{0,8},{8,0},{16,24},{24,16},{1,9},{9,1},{17,25},{25,17},{2,10},{10... | collective-permute-start | bytes 86024 | tf_op jit(solution)/shard_map/ppermute | solution.py:150

commit v2 on v0

v2 whole, which is shorter than its diff:
```python
import functools

import jax
import jax.numpy as jnp
from jax import lax
from jax.experimental import pallas as pl
from jax.experimental.pallas import tpu as pltpu
from jax.sharding import PartitionSpec as P

EPS = 1e-06
VMEM = 16 * 1024 * 1024


def dp_pairs(size, step):
    if size & (size - 1) == 0:
        return [(i, i ^ step) for i in range(size)]
    return [(i, (i + step) % size) for i in range(size)]


def order_of(size):
    return [(size - 1 - i) ^ 1 for i in range(size)]


def dp_target(size, step, me):
    if size & (size - 1) == 0:
        return jnp.bitwise_xor(me, step)
    return lax.rem(me + step, size)


def unit_of(raw):
    values = raw.astype(jnp.float32)
    inverse = lax.rsqrt(jnp.mean(values * values, axis=-1, keepdims=True) + EPS)
    return values * inverse, inverse


def contract_cols(left, right):
    return lax.dot_general(
        left, right, (((1,), (1,)), ((), ())), preferred_element_type=jnp.float32
    )


def contract_rows(left, right):
    return lax.dot_general(
        left, right, (((0,), (0,)), ((), ())), preferred_element_type=jnp.float32
    )


def fetched(kernel, inputs, outputs, *refs):
    sources, outs, scratch = refs[:inputs], refs[inputs : inputs + outputs], refs[inputs + outputs :]
    held, sems = scratch[:inputs], scratch[inputs]
    copies = [pltpu.make_async_copy(a, b, sems.at[i]) for i, (a, b) in enumerate(zip(sources, held))]
    for copy in copies:
        copy.start()
    kernel([copy.wait for copy in copies], *held, *outs, *scratch[inputs + 1 :])


def norm_kernel(n_dp, waits, q_lat, kv_lat, q_gain, kv_gain, grad_q, grad_kv, *outs):
    slices, messages = outs[-1], outs[:-1]
    for wait in waits:
        wait()
    own, q_width = q_lat.shape
    kv_width = kv_lat.shape[1]
    tokens, q_cols = grad_q.shape
    cols = q_cols + grad_kv.shape[1]
    q_rows, kv_rows = q_width // n_dp, kv_width // n_dp
    q_normed = (q_gain[...][None] * unit_of(q_lat[...])[0]).astype(jnp.bfloat16)
    kv_normed = (kv_gain[...][None] * unit_of(kv_lat[...])[0]).astype(jnp.bfloat16)
    for d in range(n_dp):
        slices[d] = jnp.concatenate(
            (q_normed[:, d * q_rows : (d + 1) * q_rows], kv_normed[:, d * kv_rows : (d + 1) * kv_rows]), axis=1
        )
    me = lax.axis_index("dp")
    for step, message in enumerate(messages):
        piece = slices[dp_target(n_dp, step, me)]
        message[:tokens, :q_cols] = grad_q[...]
        message[:tokens, q_cols:cols] = grad_kv[...]
        width = message.shape[1] - cols
        for i in range((q_rows + kv_rows) // width):
            message[i * own : (i + 1) * own, cols:] = piece[:, i * width : (i + 1) * width]


def part_kernel(order, waits, grad_q, grad_kv, kv_up, q_up, out):
    own = out.shape[1]
    q_width, kv_width = q_up.shape[0], kv_up.shape[0]
    width = q_width + kv_width
    waits[0]()
    waits[1]()
    for at, grad, up, wait in ((q_width, grad_kv, kv_up, waits[2]), (0, grad_q, q_up, waits[3])):
        wait()
        value = contract_cols(grad[...], up[...])
        size = value.shape[1]
        high = value.astype(jnp.bfloat16)
        low = (value - high.astype(jnp.float32)).astype(jnp.bfloat16)
        for to, t in enumerate(order):
            rows = slice(t * own, (t + 1) * own)
            out[to, :, at : at + size] = high[rows]
            out[to, :, width + at : width + at + size] = low[rows]


def pack_kernel(n_dp, cols, start, rows, *refs):
    messages, out = refs[:n_dp], refs[-1]
    n_tensor, own = out.shape[:2]
    width = messages[0].shape[1] - cols
    for s, message in enumerate(messages):
        for i in range(rows // width):
            piece = message[i * own : (i + 1) * own, cols:]
            at = start + s * rows + i * width
            out[:, :, at : at + width] = jnp.broadcast_to(piece[None], (n_tensor,) + piece.shape)


def final_kernel(n_dp, cols, order, q_lat, kv_lat, q_gain, kv_gain, came, *refs):
    messages, (q_out, kv_out, q_weight, kv_weight) = refs[:n_dp], refs[n_dp:]
    n_tensor, own, _ = came.shape
    q_width, kv_width = q_lat.shape[1], kv_lat.shape[1]
    width = q_width + kv_width
    q_rows, q_cols = q_weight.shape
    rows = q_rows + kv_weight.shape[0]
    tokens = n_tensor * own
    normed, grads = [], []
    for s in range(n_dp):
        at = 2 * width + s * rows
        normed += [came[order.index(t), :, at : at + rows] for t in range(n_tensor)]
        grads.append(messages[s][:tokens, :cols])
    normed = jnp.concatenate(normed, axis=0)
    grads = jnp.concatenate(grads, axis=0)
    q_weight[...] = contract_rows(normed[:, :q_rows], grads[:, :q_cols])
    kv_weight[...] = contract_rows(normed[:, q_rows:], grads[:, q_cols:])
    summed = jnp.sum(
        came[:, :, :width].astype(jnp.float32) + came[:, :, width : 2 * width].astype(jnp.float32), axis=0
    )
    for out, raw, gain, incoming in (
        (q_out, q_lat, q_gain, summed[:, :q_width]),
        (kv_out, kv_lat, kv_gain, summed[:, q_width:]),
    ):
        unit, inverse = unit_of(raw[...])
        scaled = gain[...][None] * incoming
        out[...] = inverse * (scaled - unit * jnp.mean(scaled * unit, axis=-1, keepdims=True))


def call_fetched(kernel, name, flops, out_shape, inputs, scratch_shapes=()):
    outs = len(out_shape) if isinstance(out_shape, (list, tuple)) else 1
    return call(
        functools.partial(fetched, kernel, len(inputs), outs),
        name,
        flops,
        out_shape,
        in_specs=[pl.BlockSpec(memory_space=pltpu.HBM)] * len(inputs),
        scratch_shapes=[pltpu.VMEM(x.shape, x.dtype) for x in inputs]
        + [pltpu.SemaphoreType.DMA((len(inputs),))]
        + list(scratch_shapes),
    )(*[pltpu.with_memory_space_constraint(x, pltpu.HBM) for x in inputs])


def call(kernel, name, flops, out_shape, **kwargs):
    return pl.pallas_call(
        kernel,
        out_shape=out_shape,
        cost_estimate=pl.CostEstimate(flops=flops, bytes_accessed=1000000, transcendentals=0),
        compiler_params=pltpu.CompilerParams(vmem_limit_bytes=VMEM),
        name=name,
        **kwargs,
    )


def struct(shape, dtype=jnp.float32):
    return jax.ShapeDtypeStruct(shape, dtype)


def body(n_dp, n_tensor, q_lat, kv_lat, q_gain, kv_gain, q_up, kv_up, grad_q, grad_kv):
    own, q_width = q_lat.shape
    kv_width = kv_lat.shape[1]
    tokens, q_cols = grad_q.shape
    kv_cols = grad_kv.shape[1]
    q_rows, kv_rows = q_width // n_dp, kv_width // n_dp
    rows, width, cols = q_rows + kv_rows, q_width + kv_width, q_cols + kv_cols
    extra = min(128, rows)
    messages = call_fetched(
        functools.partial(norm_kernel, n_dp),
        "norm",
        1000000,
        [struct((tokens, cols + extra), jnp.bfloat16)] * n_dp,
        (q_lat, kv_lat, q_gain, kv_gain, grad_q, grad_kv),
        [pltpu.VMEM((n_dp, own, rows), jnp.bfloat16)],
    )
    messages = [messages[0]] + [
        lax.ppermute(messages[s], "dp", dp_pairs(n_dp, s)) for s in range(1, n_dp)
    ]
    shape = struct((n_tensor, own, 2 * width + n_dp * rows), jnp.bfloat16)
    order = order_of(n_tensor)
    packed = call_fetched(
        functools.partial(part_kernel, order),
        "part",
        2 * tokens * (q_cols * q_width + kv_cols * kv_width),
        shape,
        (grad_q, grad_kv, kv_up, q_up),
    )
    packed = call(
        functools.partial(pack_kernel, n_dp, cols, 2 * width, rows),
        "pack",
        100000,
        shape,
        input_output_aliases={n_dp: 0},
    )(*messages, packed)
    came = lax.all_to_all(packed, "tensor", 0, 0, axis_index_groups=[order])
    return call(
        functools.partial(final_kernel, n_dp, cols, order),
        "final",
        2 * n_dp * tokens * (q_rows * q_cols + kv_rows * kv_cols),
        (
            struct(q_lat.shape),
            struct(kv_lat.shape),
            struct((q_rows, q_cols)),
            struct((kv_rows, kv_cols)),
        ),
    )(q_lat, kv_lat, q_gain, kv_gain, came, *messages)


def solution(mesh):
    n_dp, n_tensor = mesh.shape["dp"], mesh.shape["tensor"]
    return jax.shard_map(
        functools.partial(body, n_dp, n_tensor),
        mesh=mesh,
        in_specs=(
            P(("dp", "tensor"), None),
            P(("dp", "tensor"), None),
            P(),
            P(),
            P(None, "tensor"),
            P(None, "tensor"),
            P("dp", "tensor"),
            P("dp", "tensor"),
        ),
        out_specs=(
            P(("dp", "tensor"), None),
            P(("dp", "tensor"), None),
            P("dp", "tensor"),
            P("dp", "tensor"),
        ),
        check_vma=False,
    )
```

time: 114 us -> 21.3 us (0.19)
  blocking collectives: 58.7 us -> 11.4 us
  waiting for transfers between devices: 25.3 us -> 1.35 us
  between operations: 16.3 us -> 0.68 us
  other arithmetic: 5.96 us -> 0 us
  matrix products: 4.73 us -> 0 us
  Pallas kernels: 0 us -> 4.18 us
  starting transfers between devices: 0.13 us -> 3.26 us
  local copies, waits for them, and re-layouts: 2.45 us -> 0.01 us
    all_gather x2 -> x0, blocking collectives: 58.7 us -> none  [the longest x1 30.8 us: body(): lax.all_gather(query_latent, 'tensor', axis=0, tiled=True)]
    reduce_scatter x2 -> x0, waiting for transfers between devices: 15.9 us -> none  [the longest x1 15.9 us: body(): lax.psum_scatter(part_q, 'dp', scatter_dimension=0, tiled=True)]
    all_to_all x0 -> x1, blocking collectives: none -> 11.4 us  [body(): came = lax.all_to_all(packed, 'tensor', 0, 0, axis_index_groups=[order])]
    unnamed x4 -> x0, waiting for transfers between devices: 9.45 us -> none
    dot_general x4 -> x0, matrix products: 4.73 us -> none  [the longest x2 3.37 us: contract_rows(): lax.dot_general(left, right, (((0,), (0,)), ((), ())), preferred_element_...]
    pallas_call x0 -> x4, Pallas kernels: none -> 4.18 us  [the longest x2 2.91 us: call_fetched(): call(functools.partial(fetched, kernel, len(inputs), outs), name, flops,...]
    ppermute x0 -> x3, starting transfers between devices: none -> 3.26 us  [body(): lax.ppermute(messages[s], 'dp', dp_pairs(n_dp, s))]
    mul x2 -> x0, other arithmetic: 2.87 us -> none  [backward_of_norm(): return inverse_norm * (scaled_gradient - unit_input * mean_correction)]
  transfers between devices with their start and end apart: 3 -> 3, of which waited for: 2 -> 1; matrix products, arithmetic and copies ran while one was open for 8% -> 0% of each run, Pallas kernels for 0% -> 9%
where the time goes in v2:
time: 21.3 us; the launch traced here: 20.9 us
  blocking collectives  11.4 us (54%)
  Pallas kernels  4.18 us (20%)
  starting transfers between devices  3.26 us (15%)
  waiting for transfers between devices  1.35 us (6%)
  between operations  0.68 us (3%)
    all_to_all x1, blocking collectives, body(): came = lax.all_to_all(packed, 'tensor', 0, 0, axis_index_groups=[order])  11.4 us
    ppermute x3, starting transfers between devices, body(): lax.ppermute(messages[s], 'dp', dp_pairs(n_dp, s))  3.26 us
    pallas_call x2, Pallas kernels, call_fetched(): call(functools.partial(fetched, kernel, len(inputs), outs), name, flops,...  2.91 us
    ppermute x3, waiting for transfers between devices, body(): lax.ppermute(messages[s], 'dp', dp_pairs(n_dp, s))  1.35 us
    pallas_call x1, Pallas kernels, body(): call(functools.partial(final_kernel, n_dp, cols, order), 'final', 2 * n_d...  1.23 us
  transfers between devices with their start and end apart: 3, of which 1 were waited for; matrix products, arithmetic and copies ran while one was open for 0% of the time, Pallas kernels for 9%

profile of v2, /device:TPU:0, one launch (start us, length us, event | category | flops | bytes accessed | tf_op | source)
XLA Modules:
  0.0 20.9 jit_solution(15005848283877698892)
XLA Ops:
  0.6 1.0 %norm.1 = (bf16[16,1024]{1,0:T(8,128)(2,1)S(1)}, bf16[16,1024]{1,0:T(8,128)(2,1)S(1)}, bf16[16,1024]{1,0:T(8,128)(2,1)S(1)}, bf16[16,1024]{1,0:T(8,128)(2,1)S(1)}) custom-call(bf16[2,1536]{1,0:T(2,128)(2,1)} %q_lat.1, bf16[2,512]{1,0:T(2,128)(2,1)} %kv_lat.1, f32[1536]{0:T(1024)} %q_gain.1, f32[512]{0:T(512)} %kv_gain.1, bf16[16,384]{1,0:T(8,128)(2,1)} %refs_0_.3, ...), custom_call_target="tpu_custom_call" | custom-call | flops 1000000 | bytes 1000000 | tf_op jit(solution)/shard_map/norm/pallas_call | solution.py:142
  1.6 0.6 %collective-permute-start = (bf16[16,1024]{1,0:T(8,128)(2,1)S(1)}, bf16[16,1024]{1,0:T(8,128)(2,1)S(1)}, u32[]{:S(2)}, u32[]{:S(2)}) collective-permute-start(bf16[16,1024]{1,0:T(8,128)(2,1)S(1)} %get-tuple-element.9), channel_id=1, source_target_pairs={{0,8},{8,0},{16,24},{24,16},{1,9},{9,1},{17,25},{25,17},{2,10},{10... | collective-permute-start | bytes 98312 | tf_op jit(solution)/shard_map/ppermute | solution.py:186
  2.2 2.6 %collective-permute-start.1 = (bf16[16,1024]{1,0:T(8,128)(2,1)S(1)}, bf16[16,1024]{1,0:T(8,128)(2,1)S(1)}, u32[]{:S(2)}, u32[]{:S(2)}) collective-permute-start(bf16[16,1024]{1,0:T(8,128)(2,1)S(1)} %get-tuple-element.10), channel_id=1, source_target_pairs={{0,16},{8,24},{16,0},{24,8},{1,17},{9,25},{17,1},{25,9},{2,18},{10... | collective-permute-start | bytes 98312 | tf_op jit(solution)/shard_map/ppermute | solution.py:186
  4.8 0.0 copy-start
  4.8 0.0 copy-start.1
  4.8 0.0 copy-start.2
  4.8 0.0 copy-start.3
  4.8 0.1 collective-permute-start.2
  4.9 1.9 %part.1.refs_4_ = bf16[8,2,6144]{2,1,0:T(2,128)(2,1)S(1)} custom-call(bf16[16,384]{1,0:T(8,128)(2,1)} %refs_0_.3, bf16[16,512]{1,0:T(8,128)(2,1)} %refs_1_.3, bf16[512,512]{1,0:T(8,128)(2,1)} %refs_2_.3, bf16[1536,384]{1,0:T(8,128)(2,1)} %refs_3_.3), custom_call_target="tpu_custom_call" | custom-call | flops 27262976 | bytes 1000000 | tf_op jit(solution)/shard_map/part/pallas_call | solution.py:142
  6.8 0.0 collective-permute-done.refs_1_
  6.8 0.0 collective-permute-done.1.refs_2_
  6.8 1.3 %collective-permute-done.2.refs_3_ = bf16[16,1024]{1,0:T(8,128)(2,1)S(1)} collective-permute-done((bf16[16,1024]{1,0:T(8,128)(2,1)S(1)}, bf16[16,1024]{1,0:T(8,128)(2,1)S(1)}, u32[]{:S(2)}, u32[]{:S(2)}) %collective-permute-start.2) | collective-permute-done | bytes 32800 | tf_op jit(solution)/shard_map/ppermute | solution.py:186
  8.2 11.4 %all_to_all.5.came = bf16[8,2,6144]{2,1,0:T(2,128)(2,1)S(1)} all-to-all(bf16[8,2,6144]{2,1,0:T(2,128)(2,1)S(1)} %pack.1), channel_id=1, replica_groups={{6,7,4,5,2,3,0,1},{14,15,12,13,10,11,8,9},{22,23,20,21,18,19,16,17},{30..., dimensions={0} | all-to-all | bytes 393216 | tf_op jit(solution)/shard_map/all_to_all | solution.py:204
  19.7 0.0 copy-done
  19.7 0.0 copy-done.1
  19.7 0.0 copy-done.2
  19.7 0.0 copy-done.3
  19.7 1.2 %final.1 = (f32[2,1536]{1,0:T(2,128)}, f32[2,512]{1,0:T(2,128)}, f32[384,384]{1,0:T(8,128)}, f32[128,512]{1,0:T(8,128)}) custom-call(bf16[2,1536]{1,0:T(2,128)(2,1)S(1)} %copy-done.1, bf16[2,512]{1,0:T(2,128)(2,1)S(1)} %copy-done.2, f32[1536]{0:T(1024)S(1)} %copy-done, f32[512]{0:T(512)S(1)} %copy-done.3, bf16[8,2,6144]{2,1,0:T(2,128)(2,1)S(1)} %all_to_all.5.came, ...), custom_call_target="tpu_custom_call" | custom-call | flops 27262976 | bytes 1000000 | tf_op jit(solution)/shard_map/final/pallas_call | solution.py:205
  (1 shorter events, 0.0 us)
Async XLA Ops:
  1.6 5.2 %collective-permute-start = (bf16[16,1024]{1,0:T(8,128)(2,1)S(1)}, bf16[16,1024]{1,0:T(8,128)(2,1)S(1)}, u32[]{:S(2)}, u32[]{:S(2)}) collective-permute-start(bf16[16,1024]{1,0:T(8,128)(2,1)S(1)} %get-tuple-element.9), channel_id=1, source_target_pairs={{0,8},{8,0},{16,24},{24,16},{1,9},{9,1},{17,25},{25,17},{2,10},{10... | collective-permute-start | bytes 98312 | tf_op jit(solution)/shard_map/ppermute | solution.py:186
  2.2 4.7 %collective-permute-start.1 = (bf16[16,1024]{1,0:T(8,128)(2,1)S(1)}, bf16[16,1024]{1,0:T(8,128)(2,1)S(1)}, u32[]{:S(2)}, u32[]{:S(2)}) collective-permute-start(bf16[16,1024]{1,0:T(8,128)(2,1)S(1)} %get-tuple-element.10), channel_id=1, source_target_pairs={{0,16},{8,24},{16,0},{24,8},{1,17},{9,25},{17,1},{25,9},{2,18},{10... | collective-permute-start | bytes 98312 | tf_op jit(solution)/shard_map/ppermute | solution.py:186
  4.8 14.9 %copy-start = (f32[1536]{0:T(1024)S(1)}, f32[1536]{0:T(1024)}, u32[]{:S(2)}) copy-start(f32[1536]{0:T(1024)} %q_gain.1) | copy-start | bytes 18436
  4.8 14.9 %copy-start.1 = (bf16[2,1536]{1,0:T(2,128)(2,1)S(1)}, bf16[2,1536]{1,0:T(2,128)(2,1)}, u32[]{:S(2)}) copy-start(bf16[2,1536]{1,0:T(2,128)(2,1)} %q_lat.1) | copy-start | bytes 18436
  4.8 14.9 %copy-start.2 = (bf16[2,512]{1,0:T(2,128)(2,1)S(1)}, bf16[2,512]{1,0:T(2,128)(2,1)}, u32[]{:S(2)}) copy-start(bf16[2,512]{1,0:T(2,128)(2,1)} %kv_lat.1) | copy-start | bytes 6148
  4.8 14.9 %copy-start.3 = (f32[512]{0:T(512)S(1)}, f32[512]{0:T(512)}, u32[]{:S(2)}) copy-start(f32[512]{0:T(512)} %kv_gain.1) | copy-start | bytes 6148
  4.8 3.4 %collective-permute-start.2 = (bf16[16,1024]{1,0:T(8,128)(2,1)S(1)}, bf16[16,1024]{1,0:T(8,128)(2,1)S(1)}, u32[]{:S(2)}, u32[]{:S(2)}) collective-permute-start(bf16[16,1024]{1,0:T(8,128)(2,1)S(1)} %get-tuple-element.11), channel_id=1, source_target_pairs={{0,24},{8,16},{16,8},{24,0},{1,25},{9,17},{17,9},{25,1},{2,26},{10... | collective-permute-start | bytes 98312 | tf_op jit(solution)/shard_map/ppermute | solution.py:186
